TPU v7x, 32 devices: a whole 2x2x4 slice. The times are simulated.
32 devices in a mesh: scen: 8 (over y, x, core), own: 4 (over z).
Axes of the slice: x: 2, y: 2, z: 4, core: 2. Of those that a mesh axis runs over, the one named last changes fastest.
Arguments:
- returns: float32 [8192, 4096], P('scen', 'own'), may hold values from -50 to 50, as said below
Outputs:
- shrunk_cov: float32 [4096, 4096], P('scen', 'own')
Inputs may be any that keep to these rules, and one draw needn't show every extreme that they name: Finite real returns.
All inputs are finite; a program needn't handle non-finite values.
Results may differ from a plain program's by a relative error of at most 0.00014.
Values sent between devices are 32-bit elements; how exact they have to be, the bound alone decides.
A program may use at most 128 MiB of HBM per device.

v0:
```python
import jax
import jax.numpy as jnp
from jax import lax
from jax.sharding import PartitionSpec as P

epsilon = 1e-06


def product_over_scenarios(left_part, right_part):
    return lax.dot_general(
        left_part,
        right_part,
        (((0,), (0,)), ((), ())),
        precision=lax.Precision.HIGHEST,
        preferred_element_type=jnp.float32,
    )


def on_device(returns):
    scen_devices = lax.axis_size("scen")
    own_devices = lax.axis_size("own")
    local_rows = returns.shape[0]
    own_cols = returns.shape[1]
    scenarios = local_rows * scen_devices
    order = own_cols * own_devices
    col_total = lax.psum(jnp.sum(returns, axis=0), "scen")
    centered = returns - col_total / scenarios
    wide_rows = lax.all_gather(centered, "own", axis=1, tiled=True)
    squares = wide_rows * wide_rows
    row_norm = jnp.sum(squares, axis=1)
    beta_local = jnp.sum(row_norm * row_norm)
    trace_sum, beta_raw = lax.psum((jnp.sum(squares), beta_local), "scen")
    gram_tile = lax.psum_scatter(
        product_over_scenarios(wide_rows, centered), "scen", scatter_dimension=0, tiled=True
    )
    covariance = gram_tile / scenarios
    frob_local = jnp.sum(covariance * covariance)
    frob_sum = lax.psum(frob_local, ("scen", "own"))
    target = trace_sum / (scenarios * order)
    beta_term = (beta_raw / scenarios - frob_sum) / (order * scenarios)
    delta_term = (frob_sum - order * target * target) / order
    shrinkage = beta_term / (delta_term + epsilon)
    tile_height = covariance.shape[0]
    row_ids = lax.axis_index("scen") * tile_height + lax.broadcasted_iota(
        jnp.int32, covariance.shape, 0
    )
    col_ids = lax.axis_index("own") * own_cols + lax.broadcasted_iota(
        jnp.int32, covariance.shape, 1
    )
    diag_mask = (row_ids == col_ids).astype(jnp.float32)
    return (1.0 - shrinkage) * covariance + shrinkage * target * diag_mask


def solution(mesh):
    placed = (P("scen", "own"),)
    return jax.shard_map(
        on_device, mesh=mesh, in_specs=placed, out_specs=P("scen", "own"), check_vma=False
    )
```

profile of v0, /device:TPU:0, one launch (start us, length us, event | category | flops | bytes accessed | tf_op | source)
XLA Modules:
  0.0 543.0 jit_solution(2770630650774440942)
XLA Ops:
  6.5 0.0 all-gather.2.cloned.1.call-start
  6.5 2.5 reduce_sum.45
  9.0 15.2 %psum.28 = f32[1024]{0:T(1024)S(1)} all-reduce(f32[1024]{0:T(1024)S(1)} %reduce_sum.45), channel_id=1, replica_groups=mesh['scen'=8,'own'=4] {'scen'}, use_global_device_ids=true, to_apply=%region_1.0 | all-reduce | flops 1024 | bytes 8192 | tf_op jit(solution)/shard_map/psum | solution.py:26
  24.2 5.1 broadcast_subtract_fusion
  29.3 0.0 all-gather.2.cloned.1.call-update
  29.3 0.0 reduce-scatter.2.cloned.1.call-start
  29.3 286.2 %all-gather.2.cloned.1.call-done = f32[1024,4096]{1,0:T(8,128)} async-done(((f32[1024,1024]{1,0:T(8,128)}), f32[1024,4096]{1,0:T(8,128)}) %all-gather.2.cloned.1.call-update) | async-done | bytes 16777232 | tf_op jit(solution)/shard_map/all_gather | solution.py:28
  315.6 59.2 %fusion = f32[4096,1024]{1,0:T(8,128)} fusion(f32[1024,4096]{1,0:T(8,128)} %all-gather.2.cloned.1.call-done, f32[1024,1024]{1,0:T(8,128)} %broadcast_subtract_fusion), kind=kOutput, calls=%fused_computation.9 | convolution fusion | flops 51539607552 | bytes 37748736 | tf_op jit(solution)/shard_map/dot_general | solution.py:10
  374.8 0.0 reduce-scatter.2.cloned.1.call-update
  374.8 12.8 %multiply_reduce_fusion = (f32[]{:T(128)}, f32[1024]{0:T(1024)S(1)}) fusion(f32[1024,4096]{1,0:T(8,128)} %all-gather.2.cloned.1.call-done), kind=kLoop, calls=%fused_computation | loop fusion | flops 12581887 | bytes 16781316 | tf_op jit(solution)/shard_map/reduce_sum | solution.py:32
  387.6 0.6 multiply_reduce_fusion.3
  388.2 14.2 %all-reduce = (f32[]{:T(128)}, f32[]{:T(128)}) all-reduce(f32[]{:T(128)} %multiply_reduce_fusion.3, f32[]{:T(128)} %get-tuple-element.5), channel_id=1, replica_groups=mesh['scen'=8,'own'=4] {'scen'}, use_global_device_ids=true, to_apply=%region_5.0 | all-reduce | flops 2 | bytes 16 | tf_op jit(solution)/shard_map/psum | solution.py:32
  405.0 84.4 %reduce-scatter.2.cloned.1.call-done = f32[512,1024]{1,0:T(8,128)} async-done(((f32[4096,1024]{1,0:T(8,128)}), f32[512,1024]{1,0:T(8,128)}) %reduce-scatter.2.cloned.1.call-update) | async-done | bytes 2097168 | tf_op jit(solution)/shard_map/reduce_scatter | solution.py:33
  489.3 2.7 multiply_reduce_fusion.2
  492.1 39.5 %psum.30 = f32[]{:T(128)} all-reduce(f32[]{:T(128)} %multiply_reduce_fusion.2), channel_id=1, replica_groups=mesh['scen'=8,'own'=4] {'scen','own'}, use_global_device_ids=true, to_apply=%region_7.0 | all-reduce | flops 1 | bytes 8 | tf_op jit(solution)/shard_map/psum | solution.py:38
  532.9 3.2 select_add_fusion
  (3 shorter events, 0.0 us)
Async XLA Ops:
  6.5 309.0 %all-gather.2.cloned.1.call-start = ((), (), s32[]{:S(2)}) async-start(), calls=%async_computation.1 | async-start | bytes 20971520 | tf_op jit(solution)/shard_map/all_gather | solution.py:28
  29.3 460.0 %reduce-scatter.2.cloned.1.call-start = ((), (), s32[]{:S(2)}) async-start(), calls=%async_computation.2 | async-start | bytes 18874368 | tf_op jit(solution)/shard_map/reduce_scatter | solution.py:33
Sparse Core Ops, SparseCore 0:
  29.4 286.1 all-gather.1
  374.9 114.3 reduce-scatter.1
where the time goes:
time: 543 us
  waiting for transfers between devices  371 us (68%)
  blocking collectives  68.9 us (13%)
  matrix products  59.2 us (11%)
  other arithmetic  27 us (5%)
  between operations  17.3 us (3%)
    all_gather x1, waiting for transfers between devices, on_device(): wide_rows = lax.all_gather(centered, 'own', axis=1, tiled=True)  286 us
    reduce_scatter x1, waiting for transfers between devices, on_device(): lax.psum_scatter(product_over_scenarios(wide_rows, centered), 'scen', sca...  84.4 us
    dot_general x1, matrix products, product_over_scenarios(): lax.dot_general(left_part, right_part, (((0,), (0,)), ((), ())), precisio...  59.2 us
    psum x1, blocking collectives, on_device(): frob_sum = lax.psum(frob_local, ('scen', 'own'))  39.5 us
    psum x1, blocking collectives, on_device(): col_total = lax.psum(jnp.sum(returns, axis=0), 'scen')  15.2 us
    psum x1, blocking collectives, on_device(): trace_sum, beta_raw = lax.psum((jnp.sum(squares), beta_local), 'scen')  14.2 us
    reduce_sum x1, other arithmetic, on_device(): trace_sum, beta_raw = lax.psum((jnp.sum(squares), beta_local), 'scen')  12.8 us
  transfers between devices with their start and end apart: 2, of which 2 were waited for; matrix products, arithmetic and copies ran while one was open for 2% of the time, Pallas kernels for 0%

commit v1 on v0

--- a/solution.py
+++ b/solution.py
@@ -25,7 +25,7 @@
     order = own_cols * own_devices
     col_total = lax.psum(jnp.sum(returns, axis=0), "scen")
     centered = returns - col_total / scenarios
-    wide_rows = lax.all_gather(centered, "own", axis=1, tiled=True)
+    wide_rows = jnp.concatenate(lax.all_gather(centered, "own"), 1)
     squares = wide_rows * wide_rows
     row_norm = jnp.sum(squares, axis=1)
     beta_local = jnp.sum(row_norm * row_norm)

time: 543 us -> 561 us (1.033)
  local copies, waits for them, and re-layouts: 0 us -> 16.4 us
    reshape x0 -> x1, local copies, waits for them, and re-layouts: none -> 16.4 us  [on_device(): wide_rows = jnp.concatenate(lax.all_gather(centered, 'own'), 1)]
where the time goes in v1:
time: 561 us
  waiting for transfers between devices  371 us (66%)
  blocking collectives  68.9 us (12%)
  matrix products  59.9 us (11%)
  other arithmetic  26.9 us (5%)
  between operations  17.3 us (3%)
  local copies, waits for them, and re-layouts  16.4 us (3%)
    all_gather x1, waiting for transfers between devices, on_device(): wide_rows = jnp.concatenate(lax.all_gather(centered, 'own'), 1)  286 us
    reduce_scatter x1, waiting for transfers between devices, on_device(): lax.psum_scatter(product_over_scenarios(wide_rows, centered), 'scen', sca...  84.9 us
    dot_general x1, matrix products, product_over_scenarios(): lax.dot_general(left_part, right_part, (((0,), (0,)), ((), ())), precisio...  59.9 us
    psum x1, blocking collectives, on_device(): frob_sum = lax.psum(frob_local, ('scen', 'own'))  39.5 us
    reshape x1, local copies, waits for them, and re-layouts, on_device(): wide_rows = jnp.concatenate(lax.all_gather(centered, 'own'), 1)  16.4 us
    psum x1, blocking collectives, on_device(): col_total = lax.psum(jnp.sum(returns, axis=0), 'scen')  15.2 us
    psum x1, blocking collectives, on_device(): trace_sum, beta_raw = lax.psum((jnp.sum(squares), beta_local), 'scen')  14.2 us
    reduce_sum x1, other arithmetic, on_device(): trace_sum, beta_raw = lax.psum((jnp.sum(squares), beta_local), 'scen')  12.8 us
  transfers between devices with their start and end apart: 2, of which 2 were waited for; matrix products, arithmetic and copies ran while one was open for 2% of the time, Pallas kernels for 0%

profile of v1, /device:TPU:0, one launch (start us, length us, event | category | flops | bytes accessed | tf_op | source)
XLA Modules:
  0.0 560.6 jit_solution(3455217905758647225)
XLA Ops:
  6.5 0.0 all-gather.3.cloned.1.call-start
  6.5 2.5 reduce_sum.45
  9.0 15.2 %psum.28 = f32[1024]{0:T(1024)S(1)} all-reduce(f32[1024]{0:T(1024)S(1)} %reduce_sum.45), channel_id=1, replica_groups=mesh['scen'=8,'own'=4] {'scen'}, use_global_device_ids=true, to_apply=%region_1.0 | all-reduce | flops 1024 | bytes 8192 | tf_op jit(solution)/shard_map/psum | solution.py:26
  24.2 5.1 broadcast_subtract_fusion
  29.2 0.0 all-gather.3.cloned.1.call-update
  29.3 0.0 reduce-scatter.2.cloned.1.call-start
  29.3 286.2 %all-gather.3.cloned.1.call-done = f32[4096,1024]{1,0:T(8,128)} async-done(((f32[1024,1024]{1,0:T(8,128)}), f32[4096,1024]{1,0:T(8,128)}) %all-gather.3.cloned.1.call-update) | async-done | bytes 16777232 | tf_op jit(solution)/shard_map/all_gather | solution.py:28
  315.5 16.4 %copy.2 = f32[1024,4,1024]{0,2,1:T(8,128)} copy(f32[1024,4,1024]{2,0,1:T(8,128)} %bitcast.6) | data formatting | bytes 33554432 | tf_op jit(solution)/shard_map/reshape | solution.py:28
  331.9 59.9 %fusion = f32[4096,1024]{1,0:T(8,128)} fusion(f32[1024,4096]{0,1:T(8,128)} %bitcast.8, f32[1024,1024]{1,0:T(8,128)} %broadcast_subtract_fusion), kind=kOutput, calls=%fused_computation.9 | convolution fusion | flops 51539607552 | bytes 37748736 | tf_op jit(solution)/shard_map/dot_general | solution.py:10
  391.8 0.0 reduce-scatter.2.cloned.1.call-update
  391.9 12.8 %multiply_reduce_fusion = (f32[]{:T(128)}, f32[1024]{0:T(1024)S(1)}) fusion(f32[1024,4,1024]{2,0,1:T(8,128)} %bitcast.7), kind=kLoop, calls=%fused_computation | loop fusion | flops 12581887 | bytes 16781316 | tf_op jit(solution)/shard_map/reduce_sum | solution.py:32
  404.7 0.6 multiply_reduce_fusion.3
  405.3 14.2 %all-reduce = (f32[]{:T(128)}, f32[]{:T(128)}) all-reduce(f32[]{:T(128)} %multiply_reduce_fusion.3, f32[]{:T(128)} %get-tuple-element.5), channel_id=1, replica_groups=mesh['scen'=8,'own'=4] {'scen'}, use_global_device_ids=true, to_apply=%region_5.0 | all-reduce | flops 2 | bytes 16 | tf_op jit(solution)/shard_map/psum | solution.py:32
  421.5 84.9 %reduce-scatter.2.cloned.1.call-done = f32[512,1024]{1,0:T(8,128)} async-done(((f32[4096,1024]{1,0:T(8,128)}), f32[512,1024]{1,0:T(8,128)}) %reduce-scatter.2.cloned.1.call-update) | async-done | bytes 2097168 | tf_op jit(solution)/shard_map/reduce_scatter | solution.py:33
  506.4 2.7 multiply_reduce_fusion.2
  509.7 39.5 %psum.30 = f32[]{:T(128)} all-reduce(f32[]{:T(128)} %multiply_reduce_fusion.2), channel_id=1, replica_groups=mesh['scen'=8,'own'=4] {'scen','own'}, use_global_device_ids=true, to_apply=%region_7.0 | all-reduce | flops 1 | bytes 8 | tf_op jit(solution)/shard_map/psum | solution.py:38
  550.6 3.2 select_add_fusion
  (3 shorter events, 0.0 us)
Async XLA Ops:
  6.5 309.0 %all-gather.3.cloned.1.call-start = ((), (), s32[]{:S(2)}) async-start(), calls=%async_computation.2 | async-start | bytes 20971520 | tf_op jit(solution)/shard_map/all_gather | solution.py:28
  29.3 477.1 %reduce-scatter.2.cloned.1.call-start = ((), (), s32[]{:S(2)}) async-start(), calls=%async_computation.1 | async-start | bytes 18874368 | tf_op jit(solution)/shard_map/reduce_scatter | solution.py:33
Sparse Core Ops, SparseCore 0:
  29.4 286.1 all-gather.2
  391.9 114.3 reduce-scatter.1
